TPU v7x, 128 devices: a whole 4x4x4 slice. The times are simulated.
128 devices in a mesh: row: 8 (over y, core), col: 16 (over z, x).
Axes of the slice: x: 4, y: 4, z: 4, core: 2. Of those that a mesh axis runs over, the one named last changes fastest.
Arguments:
- parent_front: float32 [8, 2048, 4, 4096], P(None, 'row', None, 'col'), may hold values from -6 to 6
- generators: bfloat16 [96, 256, 256], P('row'), may hold values from -1.5 to 1.5
- diagonal_blocks: bfloat16 [96, 256, 256], P('row'), may hold values from -6 to 6
- coupling: bfloat16 [2, 256, 256], replicated, may hold values from -0.375 to 0.375
- block_map: int32 [2, 48], replicated, may hold values from 0 to 63, as said below
- valid_rows: int32 [2, 48], replicated, may hold values from 128 to 256
Outputs:
- assembled: float32 [8, 2048, 4, 4096], P(None, 'row', None, 'col')
Inputs may be any that keep to these rules, and one draw needn't show every extreme that they name: `block_map`: for each child c and each s < 4, the child blocks s * 12 to (s + 1) * 12 - 1 map in increasing order to distinct parent blocks of the range s * 16 to (s + 1) * 16 - 1, and the parent blocks s * 16 + m * 8 of that range always receive one.
All inputs are finite; a program needn't handle non-finite values.
Results may differ from a plain program's by a relative error of at most 0.0028.
Values may be sent and summed in bfloat16 or wider, within the bound.
No kernel may reach another device: no remote copies, remote signals or barrier semaphores. Data moves between devices by JAX's collectives and lax.ppermute only.
A program may use at most 128 MiB of HBM per device.

v0:
```python
import jax
import jax.numpy as jnp
from jax import lax
from jax.experimental import pallas as pl
from jax.experimental.pallas import tpu as pltpu
from jax.sharding import PartitionSpec as P


Y, Z, X, BLK = 4, 4, 4, 256
QUART = BLK // 4
WIN, CG = 16, 12


def pairs(move):
    out = []
    for y in range(Y):
        for k in range(2):
            for z in range(Z):
                for x in range(X):
                    b = move(y, k, z, x)
                    source = (2 * y + k) * Z * X + z * X + x
                    target = (2 * (b[0] % Y) + b[1]) * Z * X + (b[2] % Z) * X + b[3] % X
                    out.append((source, target))
    return out


def shift(value, move):
    return lax.ppermute(value, ("row", "col"), pairs(move))


def where_am_i():
    row = lax.axis_index("row")
    col = lax.axis_index("col")
    return row // 2, row % 2, col // X, col % X


def keep(count, start, rows):
    ids = lax.broadcasted_iota(jnp.int32, (rows, BLK), 0) + start
    return ids < count


def pack_kernel(
    map_hbm, count_hbm, gen_hbm, diag_hbm, coup_hbm, loc_ref, rem_ref, send_ref, col_ref,
    map_ref, count_ref, gen_ref, diag_ref, coup_ref, sems,
):
    y, k, z, x = where_am_i()
    base = y * CG
    tables = [
        pltpu.make_async_copy(map_hbm, map_ref, sems.at[0]),
        pltpu.make_async_copy(count_hbm, count_ref, sems.at[1]),
    ]
    gens = pltpu.make_async_copy(gen_hbm, gen_ref, sems.at[2])
    coup = pltpu.make_async_copy(coup_hbm.at[k], coup_ref, sems.at[3])
    for copy in tables + [gens, coup]:
        copy.start()
    zero = jnp.zeros((), jnp.bfloat16)
    loc_ref[...] = jnp.zeros_like(loc_ref)
    rem_ref[...] = jnp.zeros_like(rem_ref)
    send_ref[...] = jnp.zeros_like(send_ref)
    for copy in tables:
        copy.wait()

    target = y * WIN + z * X + x
    which = jnp.int32(0)
    kept = jnp.int32(0)
    for i in range(CG):
        hit = map_ref[k, base + i] == target
        which = jnp.where(hit, i, which)
        kept = jnp.where(hit, count_ref[k, base + i], kept)
    diag = pltpu.make_async_copy(diag_hbm.at[which], diag_ref, sems.at[4])
    diag.start()
    gens.wait()
    start = pl.multiple_of(QUART * jnp.where(k == 0, x, z), QUART)
    start_theirs = pl.multiple_of(QUART * jnp.where(k == 0, z, x), QUART)

    def one(i, carry):
        w = map_ref[k, base + i] - y * WIN
        count = count_ref[k, base + i]
        mine = lax.rem(w, 2) == k
        m = w // 8
        step = lax.rem(lax.rem(w // 2, 4) - y + 4, 4)

        @pl.when(step == 0)
        def _():
            full = jnp.where(keep(count, 0, BLK), gen_ref[i], zero)

            @pl.when(mine)
            def _():
                loc_ref[m] = full

            @pl.when(jnp.logical_not(mine))
            def _():
                for part in range(4):
                    send_ref[6 + 4 * m + part] = full[QUART * part : QUART * part + QUART]

        @pl.when(step > 0)
        def _():
            at = pl.multiple_of(jnp.where(mine, start, start_theirs), QUART)
            piece = jnp.where(keep(count, at, QUART), gen_ref[i, pl.ds(at, QUART), :], zero)

            @pl.when(mine)
            def _():
                rem_ref[step - 1, m] = piece

            @pl.when(jnp.logical_not(mine))
            def _():
                send_ref[2 * (step - 1) + m] = piece

        return carry

    lax.fori_loop(0, CG, one, 0)
    coup.wait()
    full = jnp.where(keep(kept, 0, BLK), gen_ref[which], zero)
    col_ref[0] = lax.dot_general(
        coup_ref[...], full, (((0,), (1,)), ((), ())), preferred_element_type=jnp.float32
    ).astype(jnp.bfloat16)
    diag.wait()
    lanes = lax.broadcasted_iota(jnp.int32, (BLK, BLK), 1) < kept
    col_ref[1] = jnp.where(keep(kept, 0, BLK) & lanes, diag_ref[...], zero)


def fetch_kernel(par_hbm, out_ref, buf_ref, sems):
    count = buf_ref.shape[0]
    y = where_am_i()[0]
    wanted = [2 * lax.rem(y - STEPS[i // 2] + 4, 4) + i % 2 for i in range(count)]
    copies = [pltpu.make_async_copy(par_hbm.at[a], buf_ref.at[i], sems.at[i]) for i, a in enumerate(wanted)]
    for copy in copies:
        copy.start()
    for a in range(count):
        copies[a].wait()
        for b in range(4):
            for half in range(2):
                at = pl.ds(4 * half + b, BLK, stride=8)
                out_ref[a, b, :, 128 * half : 128 * half + 128] = buf_ref[a, at, :]


STEPS = (0, 1, 3, 2)


def join_kernel(
    front_ref, loc_ref, swap_ref, g0, near1, far1, g2, near3, far3,
    col_ref, colswap_ref, c1, c2, fc1, fc2, out_hbm, rows_ref, cols_ref, diag_ref, out_ref, sems,
):
    y, k, z, x = where_am_i()
    t = z * X + x
    crossing = 2 * y + k == lax.rem(t, 8)
    group = [lax.rem(y - step + 4, 4) for step in STEPS]
    count = out_ref.shape[0]
    back = lax.rem(y + 3 + 2 * k, 4)
    ahead = lax.rem(y + 1 + 2 * k, 4)
    across = lax.rem(y + 2, 4)
    homes = (
        (y, col_ref.at[0], col_ref.at[1], colswap_ref.at[0], colswap_ref.at[1]),
        (back, c1.at[0], c1.at[1], c1.at[2], c1.at[3]),
        (ahead, fc1.at[2], fc1.at[3], fc1.at[0], fc1.at[1]),
        (across, c2.at[0], c2.at[1], fc2.at[0], fc2.at[1]),
    )

    for s, proj, diag, proj2, diag2 in homes:
        cols_ref[s, :BLK] = proj[...]
        cols_ref[s, BLK:] = proj2[...]
        diag_ref[s] = diag[...].astype(jnp.float32) + diag2[...].astype(jnp.float32)

    q = jnp.where(k == 0, x, z)
    spots = [pl.multiple_of(QUART * lax.rem(q - n + 4, 4), QUART) for n in range(4)]
    copies = []
    for i in range(count):
        m = i % 2
        if i < 2:
            rows_ref[i, :, :BLK] = loc_ref[m]
            for n in range(4):
                rows_ref[i, QUART * n : QUART * n + QUART, BLK:] = swap_ref[6 + 4 * m + n]
        else:
            j = i // 2 - 1
            quarters = [g0.at[j], near1.at[j] if j < 2 else far1, g2.at[j], near3.at[j] if j < 2 else far3]
            for at, quarter in zip(spots, quarters):
                rows_ref[i, pl.ds(at, QUART), :BLK] = quarter[0, m]
                rows_ref[i, pl.ds(at, QUART), BLK:] = quarter[1, m]
        left = rows_ref[i]
        s = group[i // 2]
        amount = jnp.where(crossing & (m == t // 8), 1.0, 0.0)
        for j in range(4):
            b = lax.rem(s + j, 4)
            tile = front_ref[i, b] + jnp.dot(left, cols_ref[b], preferred_element_type=jnp.float32)
            if j == 0:
                tile = tile + amount * diag_ref[s]
            for half in range(2):
                out_ref[i, pl.ds(4 * half + b, BLK, stride=8), :] = tile[:, 128 * half : 128 * half + 128]

        copy = pltpu.make_async_copy(out_ref.at[i], out_hbm.at[2 * s + m], sems.at[i])
        copy.start()
        copies.append(copy)
    for copy in copies:
        copy.wait()


def limits(mib, flops=0, moved=0):
    return dict(
        compiler_params=pltpu.CompilerParams(vmem_limit_bytes=mib * 2**20),
        cost_estimate=pl.CostEstimate(flops=flops, bytes_accessed=moved, transcendentals=0),
    )


def assemble(parent_front, generators, diagonal_blocks, coupling, block_map, valid_rows):
    bf16 = jnp.bfloat16
    vmem = pl.BlockSpec(memory_space=pltpu.VMEM)
    hbm = pl.BlockSpec(memory_space=pltpu.HBM)
    inputs = [
        pltpu.with_memory_space_constraint(v, pltpu.HBM)
        for v in (block_map, valid_rows, generators, diagonal_blocks, coupling)
    ]
    loc, rem, send, col = pl.pallas_call(
        pack_kernel,
        out_shape=(
            jax.ShapeDtypeStruct((2, BLK, BLK), bf16),
            jax.ShapeDtypeStruct((3, 2, QUART, BLK), bf16),
            jax.ShapeDtypeStruct((14, QUART, BLK), bf16),
            jax.ShapeDtypeStruct((2, BLK, BLK), bf16),
        ),
        in_specs=[hbm] * 5,
        out_specs=(vmem,) * 4,
        scratch_shapes=[
            pltpu.SMEM(block_map.shape, jnp.int32),
            pltpu.SMEM(valid_rows.shape, jnp.int32),
            pltpu.VMEM(generators.shape, bf16),
            pltpu.VMEM((BLK, BLK), bf16),
            pltpu.VMEM((BLK, BLK), bf16),
            pltpu.SemaphoreType.DMA((5,)),
        ],
        **limits(8, 2 * BLK**3, 2**21),
    )(*inputs)

    flip = lambda y, k, z, x: (y, 1 - k, z, x)
    swap = shift(send, flip)
    colswap = shift(col, flip)
    got = {}
    for n in (1, 3, 2):
        payload = jnp.stack([rem[n - 1], swap[2 * n - 2 : 2 * n]])
        got[n] = shift(payload, lambda y, k, z, x, n=n: (y + n, k, z, x))
    both = jnp.concatenate([col, colswap])
    c1 = shift(both, lambda y, k, z, x: (y + 1 - 2 * k, k, z, x))
    c2 = shift(col, lambda y, k, z, x: (y + 2, k, z, x))
    near = jnp.stack([got[1], got[3]])
    far = got[2]
    mine = jnp.concatenate([near, far[None]])

    def gather(value, n):
        return shift(value, lambda y, k, z, x: (y, k, z + n * k, x + n * (1 - k)))

    near1 = gather(near, 1)
    near3 = gather(near, 3)
    both2 = gather(mine, 2)
    far1 = gather(far, 1)
    far3 = gather(far, 3)
    pieces = [mine, near1, far1, both2, near3, far3]
    fc1 = shift(c1, flip)
    fc2 = shift(c2, flip)

    a_count = parent_front.shape[0]
    flat = parent_front.reshape(a_count, BLK, 4, 2, 128).transpose(0, 1, 3, 2, 4).reshape(a_count, BLK * 8, 128)
    flat = pltpu.with_memory_space_constraint(flat, pltpu.HBM)
    front = pl.pallas_call(
        fetch_kernel,
        out_shape=jax.ShapeDtypeStruct((a_count, 4, BLK, BLK), jnp.float32),
        in_specs=[hbm],
        out_specs=vmem,
        scratch_shapes=[pltpu.VMEM(flat.shape, jnp.float32), pltpu.SemaphoreType.DMA((a_count,))],
        **limits(20, 10**9, 2**23),
    )(flat)
    joined = pl.pallas_call(
        join_kernel,
        out_shape=jax.ShapeDtypeStruct(flat.shape, jnp.float32),
        in_specs=[vmem] * 15,
        out_specs=hbm,
        scratch_shapes=[
            pltpu.VMEM((a_count, BLK, 2 * BLK), bf16),
            pltpu.VMEM((4, 2 * BLK, BLK), bf16),
            pltpu.VMEM((4, BLK, BLK), jnp.float32),
            pltpu.VMEM(flat.shape, jnp.float32),
            pltpu.SemaphoreType.DMA((a_count,)),
        ],
        **limits(24, 2**31, 2**24),
    )(front, loc, swap, *pieces, col, colswap, c1, c2, fc1, fc2)
    return joined.reshape(a_count, BLK, 2, 4, 128).transpose(0, 1, 3, 2, 4).reshape(parent_front.shape)


def solution(mesh):
    in_specs = (P(None, "row", None, "col"), P("row", None, None), P("row", None, None), P(), P(), P())
    out_specs = P(None, "row", None, "col")
    return jax.shard_map(assemble, mesh=mesh, in_specs=in_specs, out_specs=out_specs, check_vma=False)
```

profile of v0, /device:TPU:0, one launch (start us, length us, event | category | flops | bytes accessed | tf_op | source)
XLA Modules:
  0.0 45.4 jit_solution(15961875681606386391)
XLA Ops:
  0.0 2.3 %shard_map.65 = (bf16[2,256,256]{2,1,0:T(8,128)(2,1)S(1)}, bf16[3,2,64,256]{3,2,1,0:T(8,128)(2,1)S(1)}, bf16[14,64,256]{2,1,0:T(8,128)(2,1)S(1)}, bf16[2,256,256]{2,1,0:T(8,128)(2,1)S(1)}) custom-call(s32[2,48]{1,0:T(2,128)} %map_hbm.1, s32[2,48]{1,0:T(2,128)} %count_hbm.1, bf16[12,256,256]{2,1,0:T(8,128)(2,1)} %gen_hbm.1, bf16[12,256,256]{2,1,0:T(8,128)(2,1)} %diag_hbm.1, ...), custom_call_target="tpu_custom_call" | custom-call | flops 33554432 | bytes 2097152 | tf_op jit(solution)/shard_map/pallas_call | solution.py:212
  2.3 0.1 collective-permute-start
  2.4 0.5 %collective-permute-start.9 = (bf16[2,256,256]{2,1,0:T(8,128)(2,1)S(1)}, bf16[2,256,256]{2,1,0:T(8,128)(2,1)S(1)}, u32[]{:S(2)}, u32[]{:S(2)}) collective-permute-start(bf16[2,256,256]{2,1,0:T(8,128)(2,1)S(1)} %get-tuple-element.12.col_ref), channel_id=1, source_target_pairs={{0,16},{1,17},{2,18},{3,19},{4,20},{5,21},{6,22},{7,23},{8,24},{9,... | collective-permute-start | bytes 786440 | tf_op jit(solution)/shard_map/ppermute | solution.py:28
  2.9 3.3 %collective-permute-start.11 = (bf16[2,256,256]{2,1,0:T(8,128)(2,1)S(1)}, bf16[2,256,256]{2,1,0:T(8,128)(2,1)S(1)}, u32[]{:S(2)}, u32[]{:S(2)}) collective-permute-start(bf16[2,256,256]{2,1,0:T(8,128)(2,1)S(1)} %get-tuple-element.12.col_ref), channel_id=1, source_target_pairs={{0,64},{1,65},{2,66},{3,67},{4,68},{5,69},{6,70},{7,71},{8,72},{9,... | collective-permute-start | bytes 786440 | tf_op jit(solution)/shard_map/ppermute | solution.py:28
  6.2 0.0 collective-permute-done.9.colswap_ref
  6.3 0.7 %collective-permute-start.10 = (bf16[4,256,256]{2,1,0:T(8,128)(2,1)S(1)}, bf16[4,256,256]{2,1,0:T(8,128)(2,1)S(1)}, u32[]{:S(2)}, u32[]{:S(2)}) collective-permute-start(bf16[4,256,256]{2,1,0:T(8,128)(2,1)S(1)} %pad_maximum_fusion), channel_id=1, source_target_pairs={{0,32},{1,33},{2,34},{3,35},{4,36},{5,37},{6,38},{7,39},{8,40},{9,... | collective-permute-start | bytes 1572872 | tf_op jit(solution)/shard_map/ppermute | solution.py:28
  7.0 0.0 collective-permute-done.swap_ref
  7.1 2.6 %collective-permute-start.2 = (bf16[2,2,64,256]{3,2,1,0:T(8,128)(2,1)S(1)}, bf16[2,2,64,256]{3,2,1,0:T(8,128)(2,1)S(1)}, u32[]{:S(2)}, u32[]{:S(2)}) collective-permute-start(bf16[2,2,64,256]{3,2,1,0:T(8,128)(2,1)S(1)} %pad_maximum_fusion.4), channel_id=1, source_target_pairs={{0,96},{1,97},{2,98},{3,99},{4,100},{5,101},{6,102},{7,103},{8,104... | collective-permute-start | bytes 393224 | tf_op jit(solution)/shard_map/ppermute | solution.py:28
  9.7 0.5 %collective-permute-start.3 = (bf16[2,2,64,256]{3,2,1,0:T(8,128)(2,1)S(1)}, bf16[2,2,64,256]{3,2,1,0:T(8,128)(2,1)S(1)}, u32[]{:S(2)}, u32[]{:S(2)}) collective-permute-start(bf16[2,2,64,256]{3,2,1,0:T(8,128)(2,1)S(1)} %pad_maximum_fusion.5), channel_id=1, source_target_pairs={{0,64},{1,65},{2,66},{3,67},{4,68},{5,69},{6,70},{7,71},{8,72},{9,... | collective-permute-start | bytes 393224 | tf_op jit(solution)/shard_map/ppermute | solution.py:28
  10.3 0.7 %collective-permute-start.1 = (bf16[2,2,64,256]{3,2,1,0:T(8,128)(2,1)S(1)}, bf16[2,2,64,256]{3,2,1,0:T(8,128)(2,1)S(1)}, u32[]{:S(2)}, u32[]{:S(2)}) collective-permute-start(bf16[2,2,64,256]{3,2,1,0:T(8,128)(2,1)S(1)} %pad_maximum_fusion.3), channel_id=1, source_target_pairs={{0,32},{1,33},{2,34},{3,35},{4,36},{5,37},{6,38},{7,39},{8,40},{9,... | collective-permute-start | bytes 393224 | tf_op jit(solution)/shard_map/ppermute | solution.py:28
  11.0 2.2 %collective-permute-done.11.c2 = bf16[2,256,256]{2,1,0:T(8,128)(2,1)S(1)} collective-permute-done((bf16[2,256,256]{2,1,0:T(8,128)(2,1)S(1)}, bf16[2,256,256]{2,1,0:T(8,128)(2,1)S(1)}, u32[]{:S(2)}, u32[]{:S(2)}) %collective-permute-start.11) | collective-permute-done | bytes 262176 | tf_op jit(solution)/shard_map/ppermute | solution.py:28
  13.2 0.0 collective-permute-start.13
  13.2 8.0 %collective-permute-done.10.c1 = bf16[4,256,256]{2,1,0:T(8,128)(2,1)S(1)} collective-permute-done((bf16[4,256,256]{2,1,0:T(8,128)(2,1)S(1)}, bf16[4,256,256]{2,1,0:T(8,128)(2,1)S(1)}, u32[]{:S(2)}, u32[]{:S(2)}) %collective-permute-start.10) | collective-permute-done | bytes 524320 | tf_op jit(solution)/shard_map/ppermute | solution.py:28
  21.2 0.5 %collective-permute-start.12 = (bf16[4,256,256]{2,1,0:T(8,128)(2,1)S(1)}, bf16[4,256,256]{2,1,0:T(8,128)(2,1)S(1)}, u32[]{:S(2)}, u32[]{:S(2)}) collective-permute-start(bf16[4,256,256]{2,1,0:T(8,128)(2,1)S(1)} %collective-permute-done.10.c1), channel_id=1, source_target_pairs={{0,16},{1,17},{2,18},{3,19},{4,20},{5,21},{6,22},{7,23},{8,24},{9,... | collective-permute-start | bytes 1572872 | tf_op jit(solution)/shard_map/ppermute | solution.py:28
  21.8 0.0 collective-permute-done.2
  21.8 1.0 %collective-permute-done.3 = bf16[2,2,64,256]{3,2,1,0:T(8,128)(2,1)S(1)} collective-permute-done((bf16[2,2,64,256]{3,2,1,0:T(8,128)(2,1)S(1)}, bf16[2,2,64,256]{3,2,1,0:T(8,128)(2,1)S(1)}, u32[]{:S(2)}, u32[]{:S(2)}) %collective-permute-start.3) | collective-permute-done | bytes 131104 | tf_op jit(solution)/shard_map/ppermute | solution.py:28
  22.8 1.3 %collective-permute-done.1 = bf16[2,2,64,256]{3,2,1,0:T(8,128)(2,1)S(1)} collective-permute-done((bf16[2,2,64,256]{3,2,1,0:T(8,128)(2,1)S(1)}, bf16[2,2,64,256]{3,2,1,0:T(8,128)(2,1)S(1)}, u32[]{:S(2)}, u32[]{:S(2)}) %collective-permute-start.1) | collective-permute-done | bytes 131104 | tf_op jit(solution)/shard_map/ppermute | solution.py:28
  24.1 3.2 %collective-permute-start.6 = (bf16[3,2,2,64,256]{4,3,2,1,0:T(8,128)(2,1)S(1)}, bf16[3,2,2,64,256]{4,3,2,1,0:T(8,128)(2,1)S(1)}, u32[]{:S(2)}, u32[]{:S(2)}) collective-permute-start(bf16[3,2,2,64,256]{4,3,2,1,0:T(8,128)(2,1)S(1)} %pad_maximum_fusion.1.g0), channel_id=1, source_target_pairs={{0,2},{1,3},{2,0},{3,1},{4,6},{5,7},{6,4},{7,5},{8,10},{9,11},{10,... | collective-permute-start | bytes 1179656 | tf_op jit(solution)/shard_map/ppermute | solution.py:28
  27.3 1.2 %collective-permute-start.8 = (bf16[2,2,64,256]{3,2,1,0:T(8,128)(2,1)S(1)}, bf16[2,2,64,256]{3,2,1,0:T(8,128)(2,1)S(1)}, u32[]{:S(2)}, u32[]{:S(2)}) collective-permute-start(bf16[2,2,64,256]{3,2,1,0:T(8,128)(2,1)S(1)} %collective-permute-done.3), channel_id=1, source_target_pairs={{0,3},{1,0},{2,1},{3,2},{4,7},{5,4},{6,5},{7,6},{8,11},{9,8},{10,9... | collective-permute-start | bytes 393224 | tf_op jit(solution)/shard_map/ppermute | solution.py:28
  28.5 0.1 collective-permute-start.7
  28.6 0.0 collective-permute-done.13.fc2
  28.6 1.9 %collective-permute-start.4 = (bf16[2,2,2,64,256]{4,3,2,1,0:T(8,128)(2,1)S(1)}, bf16[2,2,2,64,256]{4,3,2,1,0:T(8,128)(2,1)S(1)}, u32[]{:S(2)}, u32[]{:S(2)}) collective-permute-start(bf16[2,2,2,64,256]{4,3,2,1,0:T(8,128)(2,1)S(1)} %pad_maximum_fusion.2), channel_id=1, source_target_pairs={{0,1},{1,2},{2,3},{3,0},{4,5},{5,6},{6,7},{7,4},{8,9},{9,10},{10,1... | collective-permute-start | bytes 786440 | tf_op jit(solution)/shard_map/ppermute | solution.py:28
  30.5 4.5 %collective-permute-done.8.far3 = bf16[2,2,64,256]{3,2,1,0:T(8,128)(2,1)S(1)} collective-permute-done((bf16[2,2,64,256]{3,2,1,0:T(8,128)(2,1)S(1)}, bf16[2,2,64,256]{3,2,1,0:T(8,128)(2,1)S(1)}, u32[]{:S(2)}, u32[]{:S(2)}) %collective-permute-start.8) | collective-permute-done | bytes 131104 | tf_op jit(solution)/shard_map/ppermute | solution.py:28
  35.0 1.4 %collective-permute-start.5 = (bf16[2,2,64,256]{3,2,1,0:T(8,128)(2,1)S(1)}, bf16[2,2,64,256]{3,2,1,0:T(8,128)(2,1)S(1)}, u32[]{:S(2)}, u32[]{:S(2)}) collective-permute-start(bf16[2,2,64,256]{3,2,1,0:T(8,128)(2,1)S(1)} %collective-permute-done.3), channel_id=1, source_target_pairs={{0,1},{1,2},{2,3},{3,0},{4,5},{5,6},{6,7},{7,4},{8,9},{9,10},{10,1... | collective-permute-start | bytes 393224 | tf_op jit(solution)/shard_map/ppermute | solution.py:28
  36.4 3.7 %shard_map.64.front_ref = f32[8,4,256,256]{3,2,1,0:T(8,128)S(1)} custom-call(f32[8,2048,128]{2,1,0:T(8,128)} %bitcast.19), custom_call_target="tpu_custom_call" | custom-call | flops 1000000000 | bytes 8388608 | tf_op jit(solution)/shard_map/pallas_call | solution.py:262
  40.1 1.1 %collective-permute-done.5.far1 = bf16[2,2,64,256]{3,2,1,0:T(8,128)(2,1)S(1)} collective-permute-done((bf16[2,2,64,256]{3,2,1,0:T(8,128)(2,1)S(1)}, bf16[2,2,64,256]{3,2,1,0:T(8,128)(2,1)S(1)}, u32[]{:S(2)}, u32[]{:S(2)}) %collective-permute-start.5) | collective-permute-done | bytes 131104 | tf_op jit(solution)/shard_map/ppermute | solution.py:28
  41.2 0.0 collective-permute-done.7.near3
  41.2 0.0 collective-permute-done.4.near1
  41.2 0.0 collective-permute-done.6.g2
  41.2 0.0 collective-permute-done.12.fc1
  41.2 4.2 %shard_map.66 = f32[8,2048,128]{2,1,0:T(8,128)} custom-call(f32[8,4,256,256]{3,2,1,0:T(8,128)S(1)} %shard_map.64.front_ref, bf16[2,256,256]{2,1,0:T(8,128)(2,1)S(1)} %get-tuple-element.9.loc_ref, bf16[14,64,256]{2,1,0:T(8,128)(2,1)S(1)} %collective-permute-done.swap_ref, bf16[3,2,2,64,256]{4,3,2,1,0:T(8,128)(2,1)S(1)} %pad_maximum_fusion.1.g0, ...), custom_call_target="tpu_custom_call" | custom-call | flops 2147483648 | bytes 16777216 | tf_op jit(solution)/shard_map/pallas_call | solution.py:270
  (8 shorter events, 0.2 us)
Async XLA Ops:
  2.3 4.7 %collective-permute-start = (bf16[14,64,256]{2,1,0:T(8,128)(2,1)S(1)}, bf16[14,64,256]{2,1,0:T(8,128)(2,1)S(1)}, u32[]{:S(2)}, u32[]{:S(2)}) collective-permute-start(bf16[14,64,256]{2,1,0:T(8,128)(2,1)S(1)} %get-tuple-element.10), channel_id=1, source_target_pairs={{0,16},{1,17},{2,18},{3,19},{4,20},{5,21},{6,22},{7,23},{8,24},{9,... | collective-permute-start | bytes 1376264 | tf_op jit(solution)/shard_map/ppermute | solution.py:28
  2.4 3.8 %collective-permute-start.9 = (bf16[2,256,256]{2,1,0:T(8,128)(2,1)S(1)}, bf16[2,256,256]{2,1,0:T(8,128)(2,1)S(1)}, u32[]{:S(2)}, u32[]{:S(2)}) collective-permute-start(bf16[2,256,256]{2,1,0:T(8,128)(2,1)S(1)} %get-tuple-element.12.col_ref), channel_id=1, source_target_pairs={{0,16},{1,17},{2,18},{3,19},{4,20},{5,21},{6,22},{7,23},{8,24},{9,... | collective-permute-start | bytes 786440 | tf_op jit(solution)/shard_map/ppermute | solution.py:28
  2.9 10.3 %collective-permute-start.11 = (bf16[2,256,256]{2,1,0:T(8,128)(2,1)S(1)}, bf16[2,256,256]{2,1,0:T(8,128)(2,1)S(1)}, u32[]{:S(2)}, u32[]{:S(2)}) collective-permute-start(bf16[2,256,256]{2,1,0:T(8,128)(2,1)S(1)} %get-tuple-element.12.col_ref), channel_id=1, source_target_pairs={{0,64},{1,65},{2,66},{3,67},{4,68},{5,69},{6,70},{7,71},{8,72},{9,... | collective-permute-start | bytes 786440 | tf_op jit(solution)/shard_map/ppermute | solution.py:28
  6.3 14.9 %collective-permute-start.10 = (bf16[4,256,256]{2,1,0:T(8,128)(2,1)S(1)}, bf16[4,256,256]{2,1,0:T(8,128)(2,1)S(1)}, u32[]{:S(2)}, u32[]{:S(2)}) collective-permute-start(bf16[4,256,256]{2,1,0:T(8,128)(2,1)S(1)} %pad_maximum_fusion), channel_id=1, source_target_pairs={{0,32},{1,33},{2,34},{3,35},{4,36},{5,37},{6,38},{7,39},{8,40},{9,... | collective-permute-start | bytes 1572872 | tf_op jit(solution)/shard_map/ppermute | solution.py:28
  7.1 14.7 %collective-permute-start.2 = (bf16[2,2,64,256]{3,2,1,0:T(8,128)(2,1)S(1)}, bf16[2,2,64,256]{3,2,1,0:T(8,128)(2,1)S(1)}, u32[]{:S(2)}, u32[]{:S(2)}) collective-permute-start(bf16[2,2,64,256]{3,2,1,0:T(8,128)(2,1)S(1)} %pad_maximum_fusion.4), channel_id=1, source_target_pairs={{0,96},{1,97},{2,98},{3,99},{4,100},{5,101},{6,102},{7,103},{8,104... | collective-permute-start | bytes 393224 | tf_op jit(solution)/shard_map/ppermute | solution.py:28
  9.7 13.0 %collective-permute-start.3 = (bf16[2,2,64,256]{3,2,1,0:T(8,128)(2,1)S(1)}, bf16[2,2,64,256]{3,2,1,0:T(8,128)(2,1)S(1)}, u32[]{:S(2)}, u32[]{:S(2)}) collective-permute-start(bf16[2,2,64,256]{3,2,1,0:T(8,128)(2,1)S(1)} %pad_maximum_fusion.5), channel_id=1, source_target_pairs={{0,64},{1,65},{2,66},{3,67},{4,68},{5,69},{6,70},{7,71},{8,72},{9,... | collective-permute-start | bytes 393224 | tf_op jit(solution)/shard_map/ppermute | solution.py:28
  10.3 13.7 %collective-permute-start.1 = (bf16[2,2,64,256]{3,2,1,0:T(8,128)(2,1)S(1)}, bf16[2,2,64,256]{3,2,1,0:T(8,128)(2,1)S(1)}, u32[]{:S(2)}, u32[]{:S(2)}) collective-permute-start(bf16[2,2,64,256]{3,2,1,0:T(8,128)(2,1)S(1)} %pad_maximum_fusion.3), channel_id=1, source_target_pairs={{0,32},{1,33},{2,34},{3,35},{4,36},{5,37},{6,38},{7,39},{8,40},{9,... | collective-permute-start | bytes 393224 | tf_op jit(solution)/shard_map/ppermute | solution.py:28
  13.2 15.4 %collective-permute-start.13 = (bf16[2,256,256]{2,1,0:T(8,128)(2,1)S(1)}, bf16[2,256,256]{2,1,0:T(8,128)(2,1)S(1)}, u32[]{:S(2)}, u32[]{:S(2)}) collective-permute-start(bf16[2,256,256]{2,1,0:T(8,128)(2,1)S(1)} %collective-permute-done.11.c2), channel_id=1, source_target_pairs={{0,16},{1,17},{2,18},{3,19},{4,20},{5,21},{6,22},{7,23},{8,24},{9,... | collective-permute-start | bytes 786440 | tf_op jit(solution)/shard_map/ppermute | solution.py:28
  21.2 20.0 %collective-permute-start.12 = (bf16[4,256,256]{2,1,0:T(8,128)(2,1)S(1)}, bf16[4,256,256]{2,1,0:T(8,128)(2,1)S(1)}, u32[]{:S(2)}, u32[]{:S(2)}) collective-permute-start(bf16[4,256,256]{2,1,0:T(8,128)(2,1)S(1)} %collective-permute-done.10.c1), channel_id=1, source_target_pairs={{0,16},{1,17},{2,18},{3,19},{4,20},{5,21},{6,22},{7,23},{8,24},{9,... | collective-permute-start | bytes 1572872 | tf_op jit(solution)/shard_map/ppermute | solution.py:28
  24.1 17.2 %collective-permute-start.6 = (bf16[3,2,2,64,256]{4,3,2,1,0:T(8,128)(2,1)S(1)}, bf16[3,2,2,64,256]{4,3,2,1,0:T(8,128)(2,1)S(1)}, u32[]{:S(2)}, u32[]{:S(2)}) collective-permute-start(bf16[3,2,2,64,256]{4,3,2,1,0:T(8,128)(2,1)S(1)} %pad_maximum_fusion.1.g0), channel_id=1, source_target_pairs={{0,2},{1,3},{2,0},{3,1},{4,6},{5,7},{6,4},{7,5},{8,10},{9,11},{10,... | collective-permute-start | bytes 1179656 | tf_op jit(solution)/shard_map/ppermute | solution.py:28
  27.3 7.8 %collective-permute-start.8 = (bf16[2,2,64,256]{3,2,1,0:T(8,128)(2,1)S(1)}, bf16[2,2,64,256]{3,2,1,0:T(8,128)(2,1)S(1)}, u32[]{:S(2)}, u32[]{:S(2)}) collective-permute-start(bf16[2,2,64,256]{3,2,1,0:T(8,128)(2,1)S(1)} %collective-permute-done.3), channel_id=1, source_target_pairs={{0,3},{1,0},{2,1},{3,2},{4,7},{5,4},{6,5},{7,6},{8,11},{9,8},{10,9... | collective-permute-start | bytes 393224 | tf_op jit(solution)/shard_map/ppermute | solution.py:28
  28.5 12.7 %collective-permute-start.7 = (bf16[2,2,2,64,256]{4,3,2,1,0:T(8,128)(2,1)S(1)}, bf16[2,2,2,64,256]{4,3,2,1,0:T(8,128)(2,1)S(1)}, u32[]{:S(2)}, u32[]{:S(2)}) collective-permute-start(bf16[2,2,2,64,256]{4,3,2,1,0:T(8,128)(2,1)S(1)} %pad_maximum_fusion.2), channel_id=1, source_target_pairs={{0,3},{1,0},{2,1},{3,2},{4,7},{5,4},{6,5},{7,6},{8,11},{9,8},{10,9... | collective-permute-start | bytes 786440 | tf_op jit(solution)/shard_map/ppermute | solution.py:28
  28.6 12.6 %collective-permute-start.4 = (bf16[2,2,2,64,256]{4,3,2,1,0:T(8,128)(2,1)S(1)}, bf16[2,2,2,64,256]{4,3,2,1,0:T(8,128)(2,1)S(1)}, u32[]{:S(2)}, u32[]{:S(2)}) collective-permute-start(bf16[2,2,2,64,256]{4,3,2,1,0:T(8,128)(2,1)S(1)} %pad_maximum_fusion.2), channel_id=1, source_target_pairs={{0,1},{1,2},{2,3},{3,0},{4,5},{5,6},{6,7},{7,4},{8,9},{9,10},{10,1... | collective-permute-start | bytes 786440 | tf_op jit(solution)/shard_map/ppermute | solution.py:28
  35.0 6.2 %collective-permute-start.5 = (bf16[2,2,64,256]{3,2,1,0:T(8,128)(2,1)S(1)}, bf16[2,2,64,256]{3,2,1,0:T(8,128)(2,1)S(1)}, u32[]{:S(2)}, u32[]{:S(2)}) collective-permute-start(bf16[2,2,64,256]{3,2,1,0:T(8,128)(2,1)S(1)} %collective-permute-done.3), channel_id=1, source_target_pairs={{0,1},{1,2},{2,3},{3,0},{4,5},{5,6},{6,7},{7,4},{8,9},{9,10},{10,1... | collective-permute-start | bytes 393224 | tf_op jit(solution)/shard_map/ppermute | solution.py:28
where the time goes:
time: 45.6 us; the launch traced here: 45.4 us
  waiting for transfers between devices  18.1 us (40%)
  starting transfers between devices  16.8 us (37%)
  Pallas kernels  10.2 us (22%)
    ppermute x14, waiting for transfers between devices, shift(): return lax.ppermute(value, ('row', 'col'), pairs(move))  18.1 us
    ppermute x14, starting transfers between devices, shift(): return lax.ppermute(value, ('row', 'col'), pairs(move))  16.8 us
    pallas_call x1, Pallas kernels, assemble(): pl.pallas_call(join_kernel, out_shape=jax.ShapeDtypeStruct(flat.shape, jn...  4.16 us
    pallas_call x1, Pallas kernels, assemble(): pl.pallas_call(fetch_kernel, out_shape=jax.ShapeDtypeStruct((a_count, 4,...  3.67 us
    pallas_call x1, Pallas kernels, assemble(): pl.pallas_call(pack_kernel, out_shape=(jax.ShapeDtypeStruct((2, BLK, BLK)...  2.34 us
  transfers between devices with their start and end apart: 14, of which 6 were waited for; matrix products, arithmetic and copies ran while one was open for 0% of the time, Pallas kernels for 8%

commit v1 on v0

--- a/solution.py
+++ b/solution.py
@@ -41,7 +41,7 @@
 
 def pack_kernel(
     map_hbm, count_hbm, gen_hbm, diag_hbm, coup_hbm, loc_ref, rem_ref, send_ref, col_ref,
-    map_ref, count_ref, gen_ref, diag_ref, coup_ref, sems,
+    map_ref, count_ref, slot_ref, gen_ref, diag_ref, coup_ref, sems,
 ):
     y, k, z, x = where_am_i()
     base = y * CG
@@ -54,61 +54,43 @@
     for copy in tables + [gens, coup]:
         copy.start()
     zero = jnp.zeros((), jnp.bfloat16)
-    loc_ref[...] = jnp.zeros_like(loc_ref)
-    rem_ref[...] = jnp.zeros_like(rem_ref)
-    send_ref[...] = jnp.zeros_like(send_ref)
     for copy in tables:
         copy.wait()
 
-    target = y * WIN + z * X + x
-    which = jnp.int32(0)
-    kept = jnp.int32(0)
+    for w in range(WIN):
+        slot_ref[w] = -1
     for i in range(CG):
-        hit = map_ref[k, base + i] == target
-        which = jnp.where(hit, i, which)
-        kept = jnp.where(hit, count_ref[k, base + i], kept)
+        slot_ref[map_ref[k, base + i] - y * WIN] = i
+
+    def at_slot(w):
+        i = slot_ref[w]
+        block = jnp.maximum(i, 0)
+        return block, jnp.where(i >= 0, count_ref[k, base + block], 0)
+
+    which, kept = at_slot(z * X + x)
     diag = pltpu.make_async_copy(diag_hbm.at[which], diag_ref, sems.at[4])
     diag.start()
     gens.wait()
-    start = pl.multiple_of(QUART * jnp.where(k == 0, x, z), QUART)
-    start_theirs = pl.multiple_of(QUART * jnp.where(k == 0, z, x), QUART)
-
-    def one(i, carry):
-        w = map_ref[k, base + i] - y * WIN
-        count = count_ref[k, base + i]
-        mine = lax.rem(w, 2) == k
-        m = w // 8
-        step = lax.rem(lax.rem(w // 2, 4) - y + 4, 4)
-
-        @pl.when(step == 0)
-        def _():
-            full = jnp.where(keep(count, 0, BLK), gen_ref[i], zero)
-
-            @pl.when(mine)
-            def _():
-                loc_ref[m] = full
-
-            @pl.when(jnp.logical_not(mine))
-            def _():
-                for part in range(4):
-                    send_ref[6 + 4 * m + part] = full[QUART * part : QUART * part + QUART]
-
-        @pl.when(step > 0)
-        def _():
-            at = pl.multiple_of(jnp.where(mine, start, start_theirs), QUART)
-            piece = jnp.where(keep(count, at, QUART), gen_ref[i, pl.ds(at, QUART), :], zero)
-
-            @pl.when(mine)
-            def _():
-                rem_ref[step - 1, m] = piece
-
-            @pl.when(jnp.logical_not(mine))
-            def _():
-                send_ref[2 * (step - 1) + m] = piece
-
-        return carry
-
-    lax.fori_loop(0, CG, one, 0)
+    starts = (QUART * jnp.where(k == 0, x, z), QUART * jnp.where(k == 0, z, x))
+    for step in range(4):
+        chip = lax.rem(y + step, 4)
+        for theirs in range(2):
+            start = pl.multiple_of(starts[theirs], QUART)
+            for m in range(2):
+                i, count = at_slot(8 * m + 2 * chip + (k if theirs == 0 else 1 - k))
+                if step == 0:
+                    full = jnp.where(keep(count, 0, BLK), gen_ref[i], zero)
+                    if theirs == 0:
+                        loc_ref[m] = full
+                    else:
+                        for part in range(4):
+                            send_ref[6 + 4 * m + part] = full[QUART * part : QUART * part + QUART]
+                else:
+                    piece = jnp.where(keep(count, start, QUART), gen_ref[i, pl.ds(start, QUART), :], zero)
+                    if theirs == 0:
+                        rem_ref[step - 1, m] = piece
+                    else:
+                        send_ref[2 * (step - 1) + m] = piece
     coup.wait()
     full = jnp.where(keep(kept, 0, BLK), gen_ref[which], zero)
     col_ref[0] = lax.dot_general(
@@ -222,6 +204,7 @@
         scratch_shapes=[
             pltpu.SMEM(block_map.shape, jnp.int32),
             pltpu.SMEM(valid_rows.shape, jnp.int32),
+            pltpu.SMEM((WIN,), jnp.int32),
             pltpu.VMEM(generators.shape, bf16),
             pltpu.VMEM((BLK, BLK), bf16),
             pltpu.VMEM((BLK, BLK), bf16),

time: 45.6 us -> 45.2 us (level)
  Pallas kernels: 10.2 us -> 9.71 us
where the time goes in v1:
time: 45.2 us; the launch traced here: 44.9 us
  waiting for transfers between devices  18.1 us (40%)
  starting transfers between devices  16.8 us (37%)
  Pallas kernels  9.71 us (21%)
    ppermute x14, waiting for transfers between devices, shift(): return lax.ppermute(value, ('row', 'col'), pairs(move))  18.1 us
    ppermute x14, starting transfers between devices, shift(): return lax.ppermute(value, ('row', 'col'), pairs(move))  16.8 us
    pallas_call x1, Pallas kernels, assemble(): pl.pallas_call(join_kernel, out_shape=jax.ShapeDtypeStruct(flat.shape, jn...  4.15 us
    pallas_call x1, Pallas kernels, assemble(): pl.pallas_call(fetch_kernel, out_shape=jax.ShapeDtypeStruct((a_count, 4,...  3.67 us
    pallas_call x1, Pallas kernels, assemble(): pl.pallas_call(pack_kernel, out_shape=(jax.ShapeDtypeStruct((2, BLK, BLK)...  1.88 us
  transfers between devices with their start and end apart: 14, of which 6 were waited for; matrix products, arithmetic and copies ran while one was open for 0% of the time, Pallas kernels for 8%

profile of v1, /device:TPU:0, one launch (start us, length us, event | category | flops | bytes accessed | tf_op | source)
XLA Modules:
  0.0 44.9 jit_solution(5623905519176240068)
XLA Ops:
  0.0 1.9 %shard_map.65 = (bf16[2,256,256]{2,1,0:T(8,128)(2,1)S(1)}, bf16[3,2,64,256]{3,2,1,0:T(8,128)(2,1)S(1)}, bf16[14,64,256]{2,1,0:T(8,128)(2,1)S(1)}, bf16[2,256,256]{2,1,0:T(8,128)(2,1)S(1)}) custom-call(s32[2,48]{1,0:T(2,128)} %map_hbm.1, s32[2,48]{1,0:T(2,128)} %count_hbm.1, bf16[12,256,256]{2,1,0:T(8,128)(2,1)} %gen_hbm.1, bf16[12,256,256]{2,1,0:T(8,128)(2,1)} %diag_hbm.1, ...), custom_call_target="tpu_custom_call" | custom-call | flops 33554432 | bytes 2097152 | tf_op jit(solution)/shard_map/pallas_call | solution.py:194
  1.9 0.1 collective-permute-start
  2.0 0.5 %collective-permute-start.9 = (bf16[2,256,256]{2,1,0:T(8,128)(2,1)S(1)}, bf16[2,256,256]{2,1,0:T(8,128)(2,1)S(1)}, u32[]{:S(2)}, u32[]{:S(2)}) collective-permute-start(bf16[2,256,256]{2,1,0:T(8,128)(2,1)S(1)} %get-tuple-element.12.col_ref), channel_id=1, source_target_pairs={{0,16},{1,17},{2,18},{3,19},{4,20},{5,21},{6,22},{7,23},{8,24},{9,... | collective-permute-start | bytes 786440 | tf_op jit(solution)/shard_map/ppermute | solution.py:28
  2.5 3.3 %collective-permute-start.11 = (bf16[2,256,256]{2,1,0:T(8,128)(2,1)S(1)}, bf16[2,256,256]{2,1,0:T(8,128)(2,1)S(1)}, u32[]{:S(2)}, u32[]{:S(2)}) collective-permute-start(bf16[2,256,256]{2,1,0:T(8,128)(2,1)S(1)} %get-tuple-element.12.col_ref), channel_id=1, source_target_pairs={{0,64},{1,65},{2,66},{3,67},{4,68},{5,69},{6,70},{7,71},{8,72},{9,... | collective-permute-start | bytes 786440 | tf_op jit(solution)/shard_map/ppermute | solution.py:28
  5.8 0.0 collective-permute-done.9.colswap_ref
  5.9 0.7 %collective-permute-start.10 = (bf16[4,256,256]{2,1,0:T(8,128)(2,1)S(1)}, bf16[4,256,256]{2,1,0:T(8,128)(2,1)S(1)}, u32[]{:S(2)}, u32[]{:S(2)}) collective-permute-start(bf16[4,256,256]{2,1,0:T(8,128)(2,1)S(1)} %pad_maximum_fusion), channel_id=1, source_target_pairs={{0,32},{1,33},{2,34},{3,35},{4,36},{5,37},{6,38},{7,39},{8,40},{9,... | collective-permute-start | bytes 1572872 | tf_op jit(solution)/shard_map/ppermute | solution.py:28
  6.6 0.0 collective-permute-done.swap_ref
  6.7 2.6 %collective-permute-start.2 = (bf16[2,2,64,256]{3,2,1,0:T(8,128)(2,1)S(1)}, bf16[2,2,64,256]{3,2,1,0:T(8,128)(2,1)S(1)}, u32[]{:S(2)}, u32[]{:S(2)}) collective-permute-start(bf16[2,2,64,256]{3,2,1,0:T(8,128)(2,1)S(1)} %pad_maximum_fusion.4), channel_id=1, source_target_pairs={{0,96},{1,97},{2,98},{3,99},{4,100},{5,101},{6,102},{7,103},{8,104... | collective-permute-start | bytes 393224 | tf_op jit(solution)/shard_map/ppermute | solution.py:28
  9.3 0.5 %collective-permute-start.3 = (bf16[2,2,64,256]{3,2,1,0:T(8,128)(2,1)S(1)}, bf16[2,2,64,256]{3,2,1,0:T(8,128)(2,1)S(1)}, u32[]{:S(2)}, u32[]{:S(2)}) collective-permute-start(bf16[2,2,64,256]{3,2,1,0:T(8,128)(2,1)S(1)} %pad_maximum_fusion.5), channel_id=1, source_target_pairs={{0,64},{1,65},{2,66},{3,67},{4,68},{5,69},{6,70},{7,71},{8,72},{9,... | collective-permute-start | bytes 393224 | tf_op jit(solution)/shard_map/ppermute | solution.py:28
  9.8 0.7 %collective-permute-start.1 = (bf16[2,2,64,256]{3,2,1,0:T(8,128)(2,1)S(1)}, bf16[2,2,64,256]{3,2,1,0:T(8,128)(2,1)S(1)}, u32[]{:S(2)}, u32[]{:S(2)}) collective-permute-start(bf16[2,2,64,256]{3,2,1,0:T(8,128)(2,1)S(1)} %pad_maximum_fusion.3), channel_id=1, source_target_pairs={{0,32},{1,33},{2,34},{3,35},{4,36},{5,37},{6,38},{7,39},{8,40},{9,... | collective-permute-start | bytes 393224 | tf_op jit(solution)/shard_map/ppermute | solution.py:28
  10.6 2.2 %collective-permute-done.11.c2 = bf16[2,256,256]{2,1,0:T(8,128)(2,1)S(1)} collective-permute-done((bf16[2,256,256]{2,1,0:T(8,128)(2,1)S(1)}, bf16[2,256,256]{2,1,0:T(8,128)(2,1)S(1)}, u32[]{:S(2)}, u32[]{:S(2)}) %collective-permute-start.11) | collective-permute-done | bytes 262176 | tf_op jit(solution)/shard_map/ppermute | solution.py:28
  12.8 0.0 collective-permute-start.13
  12.8 8.0 %collective-permute-done.10.c1 = bf16[4,256,256]{2,1,0:T(8,128)(2,1)S(1)} collective-permute-done((bf16[4,256,256]{2,1,0:T(8,128)(2,1)S(1)}, bf16[4,256,256]{2,1,0:T(8,128)(2,1)S(1)}, u32[]{:S(2)}, u32[]{:S(2)}) %collective-permute-start.10) | collective-permute-done | bytes 524320 | tf_op jit(solution)/shard_map/ppermute | solution.py:28
  20.8 0.6 %collective-permute-start.12 = (bf16[4,256,256]{2,1,0:T(8,128)(2,1)S(1)}, bf16[4,256,256]{2,1,0:T(8,128)(2,1)S(1)}, u32[]{:S(2)}, u32[]{:S(2)}) collective-permute-start(bf16[4,256,256]{2,1,0:T(8,128)(2,1)S(1)} %collective-permute-done.10.c1), channel_id=1, source_target_pairs={{0,16},{1,17},{2,18},{3,19},{4,20},{5,21},{6,22},{7,23},{8,24},{9,... | collective-permute-start | bytes 1572872 | tf_op jit(solution)/shard_map/ppermute | solution.py:28
  21.3 0.0 collective-permute-done.2
  21.3 1.0 %collective-permute-done.3 = bf16[2,2,64,256]{3,2,1,0:T(8,128)(2,1)S(1)} collective-permute-done((bf16[2,2,64,256]{3,2,1,0:T(8,128)(2,1)S(1)}, bf16[2,2,64,256]{3,2,1,0:T(8,128)(2,1)S(1)}, u32[]{:S(2)}, u32[]{:S(2)}) %collective-permute-start.3) | collective-permute-done | bytes 131104 | tf_op jit(solution)/shard_map/ppermute | solution.py:28
  22.3 1.3 %collective-permute-done.1 = bf16[2,2,64,256]{3,2,1,0:T(8,128)(2,1)S(1)} collective-permute-done((bf16[2,2,64,256]{3,2,1,0:T(8,128)(2,1)S(1)}, bf16[2,2,64,256]{3,2,1,0:T(8,128)(2,1)S(1)}, u32[]{:S(2)}, u32[]{:S(2)}) %collective-permute-start.1) | collective-permute-done | bytes 131104 | tf_op jit(solution)/shard_map/ppermute | solution.py:28
  23.6 3.2 %collective-permute-start.6 = (bf16[3,2,2,64,256]{4,3,2,1,0:T(8,128)(2,1)S(1)}, bf16[3,2,2,64,256]{4,3,2,1,0:T(8,128)(2,1)S(1)}, u32[]{:S(2)}, u32[]{:S(2)}) collective-permute-start(bf16[3,2,2,64,256]{4,3,2,1,0:T(8,128)(2,1)S(1)} %pad_maximum_fusion.1.g0), channel_id=1, source_target_pairs={{0,2},{1,3},{2,0},{3,1},{4,6},{5,7},{6,4},{7,5},{8,10},{9,11},{10,... | collective-permute-start | bytes 1179656 | tf_op jit(solution)/shard_map/ppermute | solution.py:28
  26.8 1.2 %collective-permute-start.8 = (bf16[2,2,64,256]{3,2,1,0:T(8,128)(2,1)S(1)}, bf16[2,2,64,256]{3,2,1,0:T(8,128)(2,1)S(1)}, u32[]{:S(2)}, u32[]{:S(2)}) collective-permute-start(bf16[2,2,64,256]{3,2,1,0:T(8,128)(2,1)S(1)} %collective-permute-done.3), channel_id=1, source_target_pairs={{0,3},{1,0},{2,1},{3,2},{4,7},{5,4},{6,5},{7,6},{8,11},{9,8},{10,9... | collective-permute-start | bytes 393224 | tf_op jit(solution)/shard_map/ppermute | solution.py:28
  28.0 0.1 collective-permute-start.7
  28.1 0.0 collective-permute-done.13.fc2
  28.1 1.9 %collective-permute-start.4 = (bf16[2,2,2,64,256]{4,3,2,1,0:T(8,128)(2,1)S(1)}, bf16[2,2,2,64,256]{4,3,2,1,0:T(8,128)(2,1)S(1)}, u32[]{:S(2)}, u32[]{:S(2)}) collective-permute-start(bf16[2,2,2,64,256]{4,3,2,1,0:T(8,128)(2,1)S(1)} %pad_maximum_fusion.2), channel_id=1, source_target_pairs={{0,1},{1,2},{2,3},{3,0},{4,5},{5,6},{6,7},{7,4},{8,9},{9,10},{10,1... | collective-permute-start | bytes 786440 | tf_op jit(solution)/shard_map/ppermute | solution.py:28
  30.1 4.5 %collective-permute-done.8.far3 = bf16[2,2,64,256]{3,2,1,0:T(8,128)(2,1)S(1)} collective-permute-done((bf16[2,2,64,256]{3,2,1,0:T(8,128)(2,1)S(1)}, bf16[2,2,64,256]{3,2,1,0:T(8,128)(2,1)S(1)}, u32[]{:S(2)}, u32[]{:S(2)}) %collective-permute-start.8) | collective-permute-done | bytes 131104 | tf_op jit(solution)/shard_map/ppermute | solution.py:28
  34.6 1.4 %collective-permute-start.5 = (bf16[2,2,64,256]{3,2,1,0:T(8,128)(2,1)S(1)}, bf16[2,2,64,256]{3,2,1,0:T(8,128)(2,1)S(1)}, u32[]{:S(2)}, u32[]{:S(2)}) collective-permute-start(bf16[2,2,64,256]{3,2,1,0:T(8,128)(2,1)S(1)} %collective-permute-done.3), channel_id=1, source_target_pairs={{0,1},{1,2},{2,3},{3,0},{4,5},{5,6},{6,7},{7,4},{8,9},{9,10},{10,1... | collective-permute-start | bytes 393224 | tf_op jit(solution)/shard_map/ppermute | solution.py:28
  35.9 3.7 %shard_map.64.front_ref = f32[8,4,256,256]{3,2,1,0:T(8,128)S(1)} custom-call(f32[8,2048,128]{2,1,0:T(8,128)} %bitcast.19), custom_call_target="tpu_custom_call" | custom-call | flops 1000000000 | bytes 8388608 | tf_op jit(solution)/shard_map/pallas_call | solution.py:245
  39.6 1.1 %collective-permute-done.5.far1 = bf16[2,2,64,256]{3,2,1,0:T(8,128)(2,1)S(1)} collective-permute-done((bf16[2,2,64,256]{3,2,1,0:T(8,128)(2,1)S(1)}, bf16[2,2,64,256]{3,2,1,0:T(8,128)(2,1)S(1)}, u32[]{:S(2)}, u32[]{:S(2)}) %collective-permute-start.5) | collective-permute-done | bytes 131104 | tf_op jit(solution)/shard_map/ppermute | solution.py:28
  40.8 0.0 collective-permute-done.7.near3
  40.8 0.0 collective-permute-done.4.near1
  40.8 0.0 collective-permute-done.6.g2
  40.8 0.0 collective-permute-done.12.fc1
  40.8 4.2 %shard_map.66 = f32[8,2048,128]{2,1,0:T(8,128)} custom-call(f32[8,4,256,256]{3,2,1,0:T(8,128)S(1)} %shard_map.64.front_ref, bf16[2,256,256]{2,1,0:T(8,128)(2,1)S(1)} %get-tuple-element.9.loc_ref, bf16[14,64,256]{2,1,0:T(8,128)(2,1)S(1)} %collective-permute-done.swap_ref, bf16[3,2,2,64,256]{4,3,2,1,0:T(8,128)(2,1)S(1)} %pad_maximum_fusion.1.g0, ...), custom_call_target="tpu_custom_call" | custom-call | flops 2147483648 | bytes 16777216 | tf_op jit(solution)/shard_map/pallas_call | solution.py:253
  (8 shorter events, 0.2 us)
Async XLA Ops:
  1.9 4.7 %collective-permute-start = (bf16[14,64,256]{2,1,0:T(8,128)(2,1)S(1)}, bf16[14,64,256]{2,1,0:T(8,128)(2,1)S(1)}, u32[]{:S(2)}, u32[]{:S(2)}) collective-permute-start(bf16[14,64,256]{2,1,0:T(8,128)(2,1)S(1)} %get-tuple-element.10), channel_id=1, source_target_pairs={{0,16},{1,17},{2,18},{3,19},{4,20},{5,21},{6,22},{7,23},{8,24},{9,... | collective-permute-start | bytes 1376264 | tf_op jit(solution)/shard_map/ppermute | solution.py:28
  2.0 3.8 %collective-permute-start.9 = (bf16[2,256,256]{2,1,0:T(8,128)(2,1)S(1)}, bf16[2,256,256]{2,1,0:T(8,128)(2,1)S(1)}, u32[]{:S(2)}, u32[]{:S(2)}) collective-permute-start(bf16[2,256,256]{2,1,0:T(8,128)(2,1)S(1)} %get-tuple-element.12.col_ref), channel_id=1, source_target_pairs={{0,16},{1,17},{2,18},{3,19},{4,20},{5,21},{6,22},{7,23},{8,24},{9,... | collective-permute-start | bytes 786440 | tf_op jit(solution)/shard_map/ppermute | solution.py:28
  2.5 10.3 %collective-permute-start.11 = (bf16[2,256,256]{2,1,0:T(8,128)(2,1)S(1)}, bf16[2,256,256]{2,1,0:T(8,128)(2,1)S(1)}, u32[]{:S(2)}, u32[]{:S(2)}) collective-permute-start(bf16[2,256,256]{2,1,0:T(8,128)(2,1)S(1)} %get-tuple-element.12.col_ref), channel_id=1, source_target_pairs={{0,64},{1,65},{2,66},{3,67},{4,68},{5,69},{6,70},{7,71},{8,72},{9,... | collective-permute-start | bytes 786440 | tf_op jit(solution)/shard_map/ppermute | solution.py:28
  5.9 14.9 %collective-permute-start.10 = (bf16[4,256,256]{2,1,0:T(8,128)(2,1)S(1)}, bf16[4,256,256]{2,1,0:T(8,128)(2,1)S(1)}, u32[]{:S(2)}, u32[]{:S(2)}) collective-permute-start(bf16[4,256,256]{2,1,0:T(8,128)(2,1)S(1)} %pad_maximum_fusion), channel_id=1, source_target_pairs={{0,32},{1,33},{2,34},{3,35},{4,36},{5,37},{6,38},{7,39},{8,40},{9,... | collective-permute-start | bytes 1572872 | tf_op jit(solution)/shard_map/ppermute | solution.py:28
  6.7 14.7 %collective-permute-start.2 = (bf16[2,2,64,256]{3,2,1,0:T(8,128)(2,1)S(1)}, bf16[2,2,64,256]{3,2,1,0:T(8,128)(2,1)S(1)}, u32[]{:S(2)}, u32[]{:S(2)}) collective-permute-start(bf16[2,2,64,256]{3,2,1,0:T(8,128)(2,1)S(1)} %pad_maximum_fusion.4), channel_id=1, source_target_pairs={{0,96},{1,97},{2,98},{3,99},{4,100},{5,101},{6,102},{7,103},{8,104... | collective-permute-start | bytes 393224 | tf_op jit(solution)/shard_map/ppermute | solution.py:28
  9.3 13.0 %collective-permute-start.3 = (bf16[2,2,64,256]{3,2,1,0:T(8,128)(2,1)S(1)}, bf16[2,2,64,256]{3,2,1,0:T(8,128)(2,1)S(1)}, u32[]{:S(2)}, u32[]{:S(2)}) collective-permute-start(bf16[2,2,64,256]{3,2,1,0:T(8,128)(2,1)S(1)} %pad_maximum_fusion.5), channel_id=1, source_target_pairs={{0,64},{1,65},{2,66},{3,67},{4,68},{5,69},{6,70},{7,71},{8,72},{9,... | collective-permute-start | bytes 393224 | tf_op jit(solution)/shard_map/ppermute | solution.py:28
  9.8 13.7 %collective-permute-start.1 = (bf16[2,2,64,256]{3,2,1,0:T(8,128)(2,1)S(1)}, bf16[2,2,64,256]{3,2,1,0:T(8,128)(2,1)S(1)}, u32[]{:S(2)}, u32[]{:S(2)}) collective-permute-start(bf16[2,2,64,256]{3,2,1,0:T(8,128)(2,1)S(1)} %pad_maximum_fusion.3), channel_id=1, source_target_pairs={{0,32},{1,33},{2,34},{3,35},{4,36},{5,37},{6,38},{7,39},{8,40},{9,... | collective-permute-start | bytes 393224 | tf_op jit(solution)/shard_map/ppermute | solution.py:28
  12.8 15.4 %collective-permute-start.13 = (bf16[2,256,256]{2,1,0:T(8,128)(2,1)S(1)}, bf16[2,256,256]{2,1,0:T(8,128)(2,1)S(1)}, u32[]{:S(2)}, u32[]{:S(2)}) collective-permute-start(bf16[2,256,256]{2,1,0:T(8,128)(2,1)S(1)} %collective-permute-done.11.c2), channel_id=1, source_target_pairs={{0,16},{1,17},{2,18},{3,19},{4,20},{5,21},{6,22},{7,23},{8,24},{9,... | collective-permute-start | bytes 786440 | tf_op jit(solution)/shard_map/ppermute | solution.py:28
  20.8 20.0 %collective-permute-start.12 = (bf16[4,256,256]{2,1,0:T(8,128)(2,1)S(1)}, bf16[4,256,256]{2,1,0:T(8,128)(2,1)S(1)}, u32[]{:S(2)}, u32[]{:S(2)}) collective-permute-start(bf16[4,256,256]{2,1,0:T(8,128)(2,1)S(1)} %collective-permute-done.10.c1), channel_id=1, source_target_pairs={{0,16},{1,17},{2,18},{3,19},{4,20},{5,21},{6,22},{7,23},{8,24},{9,... | collective-permute-start | bytes 1572872 | tf_op jit(solution)/shard_map/ppermute | solution.py:28
  23.6 17.1 %collective-permute-start.6 = (bf16[3,2,2,64,256]{4,3,2,1,0:T(8,128)(2,1)S(1)}, bf16[3,2,2,64,256]{4,3,2,1,0:T(8,128)(2,1)S(1)}, u32[]{:S(2)}, u32[]{:S(2)}) collective-permute-start(bf16[3,2,2,64,256]{4,3,2,1,0:T(8,128)(2,1)S(1)} %pad_maximum_fusion.1.g0), channel_id=1, source_target_pairs={{0,2},{1,3},{2,0},{3,1},{4,6},{5,7},{6,4},{7,5},{8,10},{9,11},{10,... | collective-permute-start | bytes 1179656 | tf_op jit(solution)/shard_map/ppermute | solution.py:28
  26.8 7.8 %collective-permute-start.8 = (bf16[2,2,64,256]{3,2,1,0:T(8,128)(2,1)S(1)}, bf16[2,2,64,256]{3,2,1,0:T(8,128)(2,1)S(1)}, u32[]{:S(2)}, u32[]{:S(2)}) collective-permute-start(bf16[2,2,64,256]{3,2,1,0:T(8,128)(2,1)S(1)} %collective-permute-done.3), channel_id=1, source_target_pairs={{0,3},{1,0},{2,1},{3,2},{4,7},{5,4},{6,5},{7,6},{8,11},{9,8},{10,9... | collective-permute-start | bytes 393224 | tf_op jit(solution)/shard_map/ppermute | solution.py:28
  28.0 12.7 %collective-permute-start.7 = (bf16[2,2,2,64,256]{4,3,2,1,0:T(8,128)(2,1)S(1)}, bf16[2,2,2,64,256]{4,3,2,1,0:T(8,128)(2,1)S(1)}, u32[]{:S(2)}, u32[]{:S(2)}) collective-permute-start(bf16[2,2,2,64,256]{4,3,2,1,0:T(8,128)(2,1)S(1)} %pad_maximum_fusion.2), channel_id=1, source_target_pairs={{0,3},{1,0},{2,1},{3,2},{4,7},{5,4},{6,5},{7,6},{8,11},{9,8},{10,9... | collective-permute-start | bytes 786440 | tf_op jit(solution)/shard_map/ppermute | solution.py:28
  28.1 12.6 %collective-permute-start.4 = (bf16[2,2,2,64,256]{4,3,2,1,0:T(8,128)(2,1)S(1)}, bf16[2,2,2,64,256]{4,3,2,1,0:T(8,128)(2,1)S(1)}, u32[]{:S(2)}, u32[]{:S(2)}) collective-permute-start(bf16[2,2,2,64,256]{4,3,2,1,0:T(8,128)(2,1)S(1)} %pad_maximum_fusion.2), channel_id=1, source_target_pairs={{0,1},{1,2},{2,3},{3,0},{4,5},{5,6},{6,7},{7,4},{8,9},{9,10},{10,1... | collective-permute-start | bytes 786440 | tf_op jit(solution)/shard_map/ppermute | solution.py:28
  34.6 6.2 %collective-permute-start.5 = (bf16[2,2,64,256]{3,2,1,0:T(8,128)(2,1)S(1)}, bf16[2,2,64,256]{3,2,1,0:T(8,128)(2,1)S(1)}, u32[]{:S(2)}, u32[]{:S(2)}) collective-permute-start(bf16[2,2,64,256]{3,2,1,0:T(8,128)(2,1)S(1)} %collective-permute-done.3), channel_id=1, source_target_pairs={{0,1},{1,2},{2,3},{3,0},{4,5},{5,6},{6,7},{7,4},{8,9},{9,10},{10,1... | collective-permute-start | bytes 393224 | tf_op jit(solution)/shard_map/ppermute | solution.py:28

commit v2 on v1

--- a/solution.py
+++ b/solution.py
@@ -87,10 +87,12 @@
                             send_ref[6 + 4 * m + part] = full[QUART * part : QUART * part + QUART]
                 else:
                     piece = jnp.where(keep(count, start, QUART), gen_ref[i, pl.ds(start, QUART), :], zero)
+                    core = k if theirs == 0 else 1 - k
+                    turn = {1: core, 3: 1 - core, 2: 2}[step]
                     if theirs == 0:
-                        rem_ref[step - 1, m] = piece
+                        rem_ref[turn, m] = piece
                     else:
-                        send_ref[2 * (step - 1) + m] = piece
+                        send_ref[2 * turn + m] = piece
     coup.wait()
     full = jnp.where(keep(kept, 0, BLK), gen_ref[which], zero)
     col_ref[0] = lax.dot_general(
@@ -101,10 +103,15 @@
     col_ref[1] = jnp.where(keep(kept, 0, BLK) & lanes, diag_ref[...], zero)
 
 
+def groups(y, k):
+    return [y, lax.rem(y + 3 + 2 * k, 4), lax.rem(y + 1 + 2 * k, 4), lax.rem(y + 2, 4)]
+
+
 def fetch_kernel(par_hbm, out_ref, buf_ref, sems):
     count = buf_ref.shape[0]
-    y = where_am_i()[0]
-    wanted = [2 * lax.rem(y - STEPS[i // 2] + 4, 4) + i % 2 for i in range(count)]
+    y, k, _, _ = where_am_i()
+    group = groups(y, k)
+    wanted = [2 * group[i // 2] + i % 2 for i in range(count)]
     copies = [pltpu.make_async_copy(par_hbm.at[a], buf_ref.at[i], sems.at[i]) for i, a in enumerate(wanted)]
     for copy in copies:
         copy.start()
@@ -116,9 +123,6 @@
                 out_ref[a, b, :, 128 * half : 128 * half + 128] = buf_ref[a, at, :]
 
 
-STEPS = (0, 1, 3, 2)
-
-
 def join_kernel(
     front_ref, loc_ref, swap_ref, g0, near1, far1, g2, near3, far3,
     col_ref, colswap_ref, c1, c2, fc1, fc2, out_hbm, rows_ref, cols_ref, diag_ref, out_ref, sems,
@@ -126,11 +130,9 @@
     y, k, z, x = where_am_i()
     t = z * X + x
     crossing = 2 * y + k == lax.rem(t, 8)
-    group = [lax.rem(y - step + 4, 4) for step in STEPS]
+    group = groups(y, k)
     count = out_ref.shape[0]
-    back = lax.rem(y + 3 + 2 * k, 4)
-    ahead = lax.rem(y + 1 + 2 * k, 4)
-    across = lax.rem(y + 2, 4)
+    _, back, ahead, across = group
     homes = (
         (y, col_ref.at[0], col_ref.at[1], colswap_ref.at[0], colswap_ref.at[1]),
         (back, c1.at[0], c1.at[1], c1.at[2], c1.at[3]),
@@ -216,14 +218,16 @@
     flip = lambda y, k, z, x: (y, 1 - k, z, x)
     swap = shift(send, flip)
     colswap = shift(col, flip)
-    got = {}
-    for n in (1, 3, 2):
-        payload = jnp.stack([rem[n - 1], swap[2 * n - 2 : 2 * n]])
-        got[n] = shift(payload, lambda y, k, z, x, n=n: (y + n, k, z, x))
+    ways = (
+        lambda y, k, z, x: (y + 1 - 2 * k, k, z, x),
+        lambda y, k, z, x: (y - 1 + 2 * k, k, z, x),
+        lambda y, k, z, x: (y + 2, k, z, x),
+    )
+    got = [shift(jnp.stack([rem[n], swap[2 * n : 2 * n + 2]]), ways[n]) for n in range(3)]
     both = jnp.concatenate([col, colswap])
     c1 = shift(both, lambda y, k, z, x: (y + 1 - 2 * k, k, z, x))
     c2 = shift(col, lambda y, k, z, x: (y + 2, k, z, x))
-    near = jnp.stack([got[1], got[3]])
+    near = jnp.stack([got[0], got[1]])
     far = got[2]
     mine = jnp.concatenate([near, far[None]])
 

time: 45.2 us -> 45.7 us (1.011); the launches traced: 44.9 us -> 44.9 us
  no operation moved by 1% of the time
where the time goes in v2:
time: 45.7 us; the launch traced here: 44.9 us
  waiting for transfers between devices  18.1 us (40%)
  starting transfers between devices  16.8 us (37%)
  Pallas kernels  9.65 us (21%)
    ppermute x14, waiting for transfers between devices, shift(): return lax.ppermute(value, ('row', 'col'), pairs(move))  18.1 us
    ppermute x14, starting transfers between devices, shift(): return lax.ppermute(value, ('row', 'col'), pairs(move))  16.8 us
    pallas_call x1, Pallas kernels, assemble(): pl.pallas_call(join_kernel, out_shape=jax.ShapeDtypeStruct(flat.shape, jn...  4.1 us
    pallas_call x1, Pallas kernels, assemble(): pl.pallas_call(fetch_kernel, out_shape=jax.ShapeDtypeStruct((a_count, 4,...  3.67 us
    pallas_call x1, Pallas kernels, assemble(): pl.pallas_call(pack_kernel, out_shape=(jax.ShapeDtypeStruct((2, BLK, BLK)...  1.88 us
  transfers between devices with their start and end apart: 14, of which 6 were waited for; matrix products, arithmetic and copies ran while one was open for 0% of the time, Pallas kernels for 8%

profile of v2, /device:TPU:0, one launch (start us, length us, event | category | flops | bytes accessed | tf_op | source)
XLA Modules:
  0.0 44.9 jit_solution(3293346386725249437)
XLA Ops:
  0.0 1.9 %shard_map.65 = (bf16[2,256,256]{2,1,0:T(8,128)(2,1)S(1)}, bf16[3,2,64,256]{3,2,1,0:T(8,128)(2,1)S(1)}, bf16[14,64,256]{2,1,0:T(8,128)(2,1)S(1)}, bf16[2,256,256]{2,1,0:T(8,128)(2,1)S(1)}) custom-call(s32[2,48]{1,0:T(2,128)} %map_hbm.1, s32[2,48]{1,0:T(2,128)} %count_hbm.1, bf16[12,256,256]{2,1,0:T(8,128)(2,1)} %gen_hbm.1, bf16[12,256,256]{2,1,0:T(8,128)(2,1)} %diag_hbm.1, ...), custom_call_target="tpu_custom_call" | custom-call | flops 33554432 | bytes 2097152 | tf_op jit(solution)/shard_map/pallas_call | solution.py:196
  1.9 0.1 collective-permute-start
  2.0 0.5 %collective-permute-start.9 = (bf16[2,256,256]{2,1,0:T(8,128)(2,1)S(1)}, bf16[2,256,256]{2,1,0:T(8,128)(2,1)S(1)}, u32[]{:S(2)}, u32[]{:S(2)}) collective-permute-start(bf16[2,256,256]{2,1,0:T(8,128)(2,1)S(1)} %get-tuple-element.12.col_ref), channel_id=1, source_target_pairs={{0,16},{1,17},{2,18},{3,19},{4,20},{5,21},{6,22},{7,23},{8,24},{9,... | collective-permute-start | bytes 786440 | tf_op jit(solution)/shard_map/ppermute | solution.py:28
  2.5 3.3 %collective-permute-start.11 = (bf16[2,256,256]{2,1,0:T(8,128)(2,1)S(1)}, bf16[2,256,256]{2,1,0:T(8,128)(2,1)S(1)}, u32[]{:S(2)}, u32[]{:S(2)}) collective-permute-start(bf16[2,256,256]{2,1,0:T(8,128)(2,1)S(1)} %get-tuple-element.12.col_ref), channel_id=1, source_target_pairs={{0,64},{1,65},{2,66},{3,67},{4,68},{5,69},{6,70},{7,71},{8,72},{9,... | collective-permute-start | bytes 786440 | tf_op jit(solution)/shard_map/ppermute | solution.py:28
  5.8 0.0 collective-permute-done.9.colswap_ref
  5.9 0.7 %collective-permute-start.10 = (bf16[4,256,256]{2,1,0:T(8,128)(2,1)S(1)}, bf16[4,256,256]{2,1,0:T(8,128)(2,1)S(1)}, u32[]{:S(2)}, u32[]{:S(2)}) collective-permute-start(bf16[4,256,256]{2,1,0:T(8,128)(2,1)S(1)} %pad_maximum_fusion), channel_id=1, source_target_pairs={{0,32},{1,33},{2,34},{3,35},{4,36},{5,37},{6,38},{7,39},{8,40},{9,... | collective-permute-start | bytes 1572872 | tf_op jit(solution)/shard_map/ppermute | solution.py:28
  6.6 0.0 collective-permute-done.swap_ref
  6.7 2.6 %collective-permute-start.2 = (bf16[2,2,64,256]{3,2,1,0:T(8,128)(2,1)S(1)}, bf16[2,2,64,256]{3,2,1,0:T(8,128)(2,1)S(1)}, u32[]{:S(2)}, u32[]{:S(2)}) collective-permute-start(bf16[2,2,64,256]{3,2,1,0:T(8,128)(2,1)S(1)} %pad_maximum_fusion.4), channel_id=1, source_target_pairs={{0,96},{1,97},{2,98},{3,99},{4,100},{5,101},{6,102},{7,103},{8,104... | collective-permute-start | bytes 393224 | tf_op jit(solution)/shard_map/ppermute | solution.py:28
  9.3 0.5 %collective-permute-start.3 = (bf16[2,2,64,256]{3,2,1,0:T(8,128)(2,1)S(1)}, bf16[2,2,64,256]{3,2,1,0:T(8,128)(2,1)S(1)}, u32[]{:S(2)}, u32[]{:S(2)}) collective-permute-start(bf16[2,2,64,256]{3,2,1,0:T(8,128)(2,1)S(1)} %pad_maximum_fusion.5), channel_id=1, source_target_pairs={{0,64},{1,65},{2,66},{3,67},{4,68},{5,69},{6,70},{7,71},{8,72},{9,... | collective-permute-start | bytes 393224 | tf_op jit(solution)/shard_map/ppermute | solution.py:28
  9.8 0.7 %collective-permute-start.1 = (bf16[2,2,64,256]{3,2,1,0:T(8,128)(2,1)S(1)}, bf16[2,2,64,256]{3,2,1,0:T(8,128)(2,1)S(1)}, u32[]{:S(2)}, u32[]{:S(2)}) collective-permute-start(bf16[2,2,64,256]{3,2,1,0:T(8,128)(2,1)S(1)} %pad_maximum_fusion.3), channel_id=1, source_target_pairs={{0,32},{1,33},{2,34},{3,35},{4,36},{5,37},{6,38},{7,39},{8,40},{9,... | collective-permute-start | bytes 393224 | tf_op jit(solution)/shard_map/ppermute | solution.py:28
  10.6 2.6 %collective-permute-done.11.c2 = bf16[2,256,256]{2,1,0:T(8,128)(2,1)S(1)} collective-permute-done((bf16[2,256,256]{2,1,0:T(8,128)(2,1)S(1)}, bf16[2,256,256]{2,1,0:T(8,128)(2,1)S(1)}, u32[]{:S(2)}, u32[]{:S(2)}) %collective-permute-start.11) | collective-permute-done | bytes 262176 | tf_op jit(solution)/shard_map/ppermute | solution.py:28
  13.2 0.0 collective-permute-start.13
  13.2 7.6 %collective-permute-done.10.c1 = bf16[4,256,256]{2,1,0:T(8,128)(2,1)S(1)} collective-permute-done((bf16[4,256,256]{2,1,0:T(8,128)(2,1)S(1)}, bf16[4,256,256]{2,1,0:T(8,128)(2,1)S(1)}, u32[]{:S(2)}, u32[]{:S(2)}) %collective-permute-start.10) | collective-permute-done | bytes 524320 | tf_op jit(solution)/shard_map/ppermute | solution.py:28
  20.8 0.6 %collective-permute-start.12 = (bf16[4,256,256]{2,1,0:T(8,128)(2,1)S(1)}, bf16[4,256,256]{2,1,0:T(8,128)(2,1)S(1)}, u32[]{:S(2)}, u32[]{:S(2)}) collective-permute-start(bf16[4,256,256]{2,1,0:T(8,128)(2,1)S(1)} %collective-permute-done.10.c1), channel_id=1, source_target_pairs={{0,16},{1,17},{2,18},{3,19},{4,20},{5,21},{6,22},{7,23},{8,24},{9,... | collective-permute-start | bytes 1572872 | tf_op jit(solution)/shard_map/ppermute | solution.py:28
  21.3 0.0 collective-permute-done.2
  21.3 0.9 %collective-permute-done.3 = bf16[2,2,64,256]{3,2,1,0:T(8,128)(2,1)S(1)} collective-permute-done((bf16[2,2,64,256]{3,2,1,0:T(8,128)(2,1)S(1)}, bf16[2,2,64,256]{3,2,1,0:T(8,128)(2,1)S(1)}, u32[]{:S(2)}, u32[]{:S(2)}) %collective-permute-start.3) | collective-permute-done | bytes 131104 | tf_op jit(solution)/shard_map/ppermute | solution.py:28
  22.3 1.3 %collective-permute-done.1 = bf16[2,2,64,256]{3,2,1,0:T(8,128)(2,1)S(1)} collective-permute-done((bf16[2,2,64,256]{3,2,1,0:T(8,128)(2,1)S(1)}, bf16[2,2,64,256]{3,2,1,0:T(8,128)(2,1)S(1)}, u32[]{:S(2)}, u32[]{:S(2)}) %collective-permute-start.1) | collective-permute-done | bytes 131104 | tf_op jit(solution)/shard_map/ppermute | solution.py:28
  23.6 3.2 %collective-permute-start.6 = (bf16[3,2,2,64,256]{4,3,2,1,0:T(8,128)(2,1)S(1)}, bf16[3,2,2,64,256]{4,3,2,1,0:T(8,128)(2,1)S(1)}, u32[]{:S(2)}, u32[]{:S(2)}) collective-permute-start(bf16[3,2,2,64,256]{4,3,2,1,0:T(8,128)(2,1)S(1)} %pad_maximum_fusion.1.g0), channel_id=1, source_target_pairs={{0,2},{1,3},{2,0},{3,1},{4,6},{5,7},{6,4},{7,5},{8,10},{9,11},{10,... | collective-permute-start | bytes 1179656 | tf_op jit(solution)/shard_map/ppermute | solution.py:28
  26.8 1.2 %collective-permute-start.8 = (bf16[2,2,64,256]{3,2,1,0:T(8,128)(2,1)S(1)}, bf16[2,2,64,256]{3,2,1,0:T(8,128)(2,1)S(1)}, u32[]{:S(2)}, u32[]{:S(2)}) collective-permute-start(bf16[2,2,64,256]{3,2,1,0:T(8,128)(2,1)S(1)} %collective-permute-done.3), channel_id=1, source_target_pairs={{0,3},{1,0},{2,1},{3,2},{4,7},{5,4},{6,5},{7,6},{8,11},{9,8},{10,9... | collective-permute-start | bytes 393224 | tf_op jit(solution)/shard_map/ppermute | solution.py:28
  28.0 0.1 collective-permute-start.7
  28.1 0.0 collective-permute-done.13.fc2
  28.1 1.9 %collective-permute-start.4 = (bf16[2,2,2,64,256]{4,3,2,1,0:T(8,128)(2,1)S(1)}, bf16[2,2,2,64,256]{4,3,2,1,0:T(8,128)(2,1)S(1)}, u32[]{:S(2)}, u32[]{:S(2)}) collective-permute-start(bf16[2,2,2,64,256]{4,3,2,1,0:T(8,128)(2,1)S(1)} %pad_maximum_fusion.2), channel_id=1, source_target_pairs={{0,1},{1,2},{2,3},{3,0},{4,5},{5,6},{6,7},{7,4},{8,9},{9,10},{10,1... | collective-permute-start | bytes 786440 | tf_op jit(solution)/shard_map/ppermute | solution.py:28
  30.1 4.5 %collective-permute-done.8.far3 = bf16[2,2,64,256]{3,2,1,0:T(8,128)(2,1)S(1)} collective-permute-done((bf16[2,2,64,256]{3,2,1,0:T(8,128)(2,1)S(1)}, bf16[2,2,64,256]{3,2,1,0:T(8,128)(2,1)S(1)}, u32[]{:S(2)}, u32[]{:S(2)}) %collective-permute-start.8) | collective-permute-done | bytes 131104 | tf_op jit(solution)/shard_map/ppermute | solution.py:28
  34.6 1.4 %collective-permute-start.5 = (bf16[2,2,64,256]{3,2,1,0:T(8,128)(2,1)S(1)}, bf16[2,2,64,256]{3,2,1,0:T(8,128)(2,1)S(1)}, u32[]{:S(2)}, u32[]{:S(2)}) collective-permute-start(bf16[2,2,64,256]{3,2,1,0:T(8,128)(2,1)S(1)} %collective-permute-done.3), channel_id=1, source_target_pairs={{0,1},{1,2},{2,3},{3,0},{4,5},{5,6},{6,7},{7,4},{8,9},{9,10},{10,1... | collective-permute-start | bytes 393224 | tf_op jit(solution)/shard_map/ppermute | solution.py:28
  35.9 3.7 %shard_map.64.front_ref = f32[8,4,256,256]{3,2,1,0:T(8,128)S(1)} custom-call(f32[8,2048,128]{2,1,0:T(8,128)} %bitcast.19), custom_call_target="tpu_custom_call" | custom-call | flops 1000000000 | bytes 8388608 | tf_op jit(solution)/shard_map/pallas_call | solution.py:249
  39.6 1.1 %collective-permute-done.5.far1 = bf16[2,2,64,256]{3,2,1,0:T(8,128)(2,1)S(1)} collective-permute-done((bf16[2,2,64,256]{3,2,1,0:T(8,128)(2,1)S(1)}, bf16[2,2,64,256]{3,2,1,0:T(8,128)(2,1)S(1)}, u32[]{:S(2)}, u32[]{:S(2)}) %collective-permute-start.5) | collective-permute-done | bytes 131104 | tf_op jit(solution)/shard_map/ppermute | solution.py:28
  40.8 0.0 collective-permute-done.7.near3
  40.8 0.0 collective-permute-done.4.near1
  40.8 0.0 collective-permute-done.6.g2
  40.8 0.0 collective-permute-done.12.fc1
  40.8 4.1 %shard_map.66 = f32[8,2048,128]{2,1,0:T(8,128)} custom-call(f32[8,4,256,256]{3,2,1,0:T(8,128)S(1)} %shard_map.64.front_ref, bf16[2,256,256]{2,1,0:T(8,128)(2,1)S(1)} %get-tuple-element.9.loc_ref, bf16[14,64,256]{2,1,0:T(8,128)(2,1)S(1)} %collective-permute-done.swap_ref, bf16[3,2,2,64,256]{4,3,2,1,0:T(8,128)(2,1)S(1)} %pad_maximum_fusion.1.g0, ...), custom_call_target="tpu_custom_call" | custom-call | flops 2147483648 | bytes 16777216 | tf_op jit(solution)/shard_map/pallas_call | solution.py:257
  (8 shorter events, 0.2 us)
Async XLA Ops:
  1.9 4.7 %collective-permute-start = (bf16[14,64,256]{2,1,0:T(8,128)(2,1)S(1)}, bf16[14,64,256]{2,1,0:T(8,128)(2,1)S(1)}, u32[]{:S(2)}, u32[]{:S(2)}) collective-permute-start(bf16[14,64,256]{2,1,0:T(8,128)(2,1)S(1)} %get-tuple-element.10), channel_id=1, source_target_pairs={{0,16},{1,17},{2,18},{3,19},{4,20},{5,21},{6,22},{7,23},{8,24},{9,... | collective-permute-start | bytes 1376264 | tf_op jit(solution)/shard_map/ppermute | solution.py:28
  2.0 3.8 %collective-permute-start.9 = (bf16[2,256,256]{2,1,0:T(8,128)(2,1)S(1)}, bf16[2,256,256]{2,1,0:T(8,128)(2,1)S(1)}, u32[]{:S(2)}, u32[]{:S(2)}) collective-permute-start(bf16[2,256,256]{2,1,0:T(8,128)(2,1)S(1)} %get-tuple-element.12.col_ref), channel_id=1, source_target_pairs={{0,16},{1,17},{2,18},{3,19},{4,20},{5,21},{6,22},{7,23},{8,24},{9,... | collective-permute-start | bytes 786440 | tf_op jit(solution)/shard_map/ppermute | solution.py:28
  2.5 10.7 %collective-permute-start.11 = (bf16[2,256,256]{2,1,0:T(8,128)(2,1)S(1)}, bf16[2,256,256]{2,1,0:T(8,128)(2,1)S(1)}, u32[]{:S(2)}, u32[]{:S(2)}) collective-permute-start(bf16[2,256,256]{2,1,0:T(8,128)(2,1)S(1)} %get-tuple-element.12.col_ref), channel_id=1, source_target_pairs={{0,64},{1,65},{2,66},{3,67},{4,68},{5,69},{6,70},{7,71},{8,72},{9,... | collective-permute-start | bytes 786440 | tf_op jit(solution)/shard_map/ppermute | solution.py:28
  5.9 14.9 %collective-permute-start.10 = (bf16[4,256,256]{2,1,0:T(8,128)(2,1)S(1)}, bf16[4,256,256]{2,1,0:T(8,128)(2,1)S(1)}, u32[]{:S(2)}, u32[]{:S(2)}) collective-permute-start(bf16[4,256,256]{2,1,0:T(8,128)(2,1)S(1)} %pad_maximum_fusion), channel_id=1, source_target_pairs={{0,32},{1,33},{2,34},{3,35},{4,36},{5,37},{6,38},{7,39},{8,40},{9,... | collective-permute-start | bytes 1572872 | tf_op jit(solution)/shard_map/ppermute | solution.py:28
  6.7 14.7 %collective-permute-start.2 = (bf16[2,2,64,256]{3,2,1,0:T(8,128)(2,1)S(1)}, bf16[2,2,64,256]{3,2,1,0:T(8,128)(2,1)S(1)}, u32[]{:S(2)}, u32[]{:S(2)}) collective-permute-start(bf16[2,2,64,256]{3,2,1,0:T(8,128)(2,1)S(1)} %pad_maximum_fusion.4), channel_id=1, source_target_pairs={{0,96},{1,97},{2,98},{3,99},{4,100},{5,101},{6,102},{7,103},{8,104... | collective-permute-start | bytes 393224 | tf_op jit(solution)/shard_map/ppermute | solution.py:28
  9.3 13.0 %collective-permute-start.3 = (bf16[2,2,64,256]{3,2,1,0:T(8,128)(2,1)S(1)}, bf16[2,2,64,256]{3,2,1,0:T(8,128)(2,1)S(1)}, u32[]{:S(2)}, u32[]{:S(2)}) collective-permute-start(bf16[2,2,64,256]{3,2,1,0:T(8,128)(2,1)S(1)} %pad_maximum_fusion.5), channel_id=1, source_target_pairs={{0,64},{1,65},{2,66},{3,67},{4,68},{5,69},{6,70},{7,71},{8,72},{9,... | collective-permute-start | bytes 393224 | tf_op jit(solution)/shard_map/ppermute | solution.py:28
  9.8 13.7 %collective-permute-start.1 = (bf16[2,2,64,256]{3,2,1,0:T(8,128)(2,1)S(1)}, bf16[2,2,64,256]{3,2,1,0:T(8,128)(2,1)S(1)}, u32[]{:S(2)}, u32[]{:S(2)}) collective-permute-start(bf16[2,2,64,256]{3,2,1,0:T(8,128)(2,1)S(1)} %pad_maximum_fusion.3), channel_id=1, source_target_pairs={{0,32},{1,33},{2,34},{3,35},{4,36},{5,37},{6,38},{7,39},{8,40},{9,... | collective-permute-start | bytes 393224 | tf_op jit(solution)/shard_map/ppermute | solution.py:28
  13.2 14.9 %collective-permute-start.13 = (bf16[2,256,256]{2,1,0:T(8,128)(2,1)S(1)}, bf16[2,256,256]{2,1,0:T(8,128)(2,1)S(1)}, u32[]{:S(2)}, u32[]{:S(2)}) collective-permute-start(bf16[2,256,256]{2,1,0:T(8,128)(2,1)S(1)} %collective-permute-done.11.c2), channel_id=1, source_target_pairs={{0,16},{1,17},{2,18},{3,19},{4,20},{5,21},{6,22},{7,23},{8,24},{9,... | collective-permute-start | bytes 786440 | tf_op jit(solution)/shard_map/ppermute | solution.py:28
  20.8 20.0 %collective-permute-start.12 = (bf16[4,256,256]{2,1,0:T(8,128)(2,1)S(1)}, bf16[4,256,256]{2,1,0:T(8,128)(2,1)S(1)}, u32[]{:S(2)}, u32[]{:S(2)}) collective-permute-start(bf16[4,256,256]{2,1,0:T(8,128)(2,1)S(1)} %collective-permute-done.10.c1), channel_id=1, source_target_pairs={{0,16},{1,17},{2,18},{3,19},{4,20},{5,21},{6,22},{7,23},{8,24},{9,... | collective-permute-start | bytes 1572872 | tf_op jit(solution)/shard_map/ppermute | solution.py:28
  23.6 17.1 %collective-permute-start.6 = (bf16[3,2,2,64,256]{4,3,2,1,0:T(8,128)(2,1)S(1)}, bf16[3,2,2,64,256]{4,3,2,1,0:T(8,128)(2,1)S(1)}, u32[]{:S(2)}, u32[]{:S(2)}) collective-permute-start(bf16[3,2,2,64,256]{4,3,2,1,0:T(8,128)(2,1)S(1)} %pad_maximum_fusion.1.g0), channel_id=1, source_target_pairs={{0,2},{1,3},{2,0},{3,1},{4,6},{5,7},{6,4},{7,5},{8,10},{9,11},{10,... | collective-permute-start | bytes 1179656 | tf_op jit(solution)/shard_map/ppermute | solution.py:28
  26.8 7.8 %collective-permute-start.8 = (bf16[2,2,64,256]{3,2,1,0:T(8,128)(2,1)S(1)}, bf16[2,2,64,256]{3,2,1,0:T(8,128)(2,1)S(1)}, u32[]{:S(2)}, u32[]{:S(2)}) collective-permute-start(bf16[2,2,64,256]{3,2,1,0:T(8,128)(2,1)S(1)} %collective-permute-done.3), channel_id=1, source_target_pairs={{0,3},{1,0},{2,1},{3,2},{4,7},{5,4},{6,5},{7,6},{8,11},{9,8},{10,9... | collective-permute-start | bytes 393224 | tf_op jit(solution)/shard_map/ppermute | solution.py:28
  28.0 12.7 %collective-permute-start.7 = (bf16[2,2,2,64,256]{4,3,2,1,0:T(8,128)(2,1)S(1)}, bf16[2,2,2,64,256]{4,3,2,1,0:T(8,128)(2,1)S(1)}, u32[]{:S(2)}, u32[]{:S(2)}) collective-permute-start(bf16[2,2,2,64,256]{4,3,2,1,0:T(8,128)(2,1)S(1)} %pad_maximum_fusion.2), channel_id=1, source_target_pairs={{0,3},{1,0},{2,1},{3,2},{4,7},{5,4},{6,5},{7,6},{8,11},{9,8},{10,9... | collective-permute-start | bytes 786440 | tf_op jit(solution)/shard_map/ppermute | solution.py:28
  28.1 12.7 %collective-permute-start.4 = (bf16[2,2,2,64,256]{4,3,2,1,0:T(8,128)(2,1)S(1)}, bf16[2,2,2,64,256]{4,3,2,1,0:T(8,128)(2,1)S(1)}, u32[]{:S(2)}, u32[]{:S(2)}) collective-permute-start(bf16[2,2,2,64,256]{4,3,2,1,0:T(8,128)(2,1)S(1)} %pad_maximum_fusion.2), channel_id=1, source_target_pairs={{0,1},{1,2},{2,3},{3,0},{4,5},{5,6},{6,7},{7,4},{8,9},{9,10},{10,1... | collective-permute-start | bytes 786440 | tf_op jit(solution)/shard_map/ppermute | solution.py:28
  34.6 6.2 %collective-permute-start.5 = (bf16[2,2,64,256]{3,2,1,0:T(8,128)(2,1)S(1)}, bf16[2,2,64,256]{3,2,1,0:T(8,128)(2,1)S(1)}, u32[]{:S(2)}, u32[]{:S(2)}) collective-permute-start(bf16[2,2,64,256]{3,2,1,0:T(8,128)(2,1)S(1)} %collective-permute-done.3), channel_id=1, source_target_pairs={{0,1},{1,2},{2,3},{3,0},{4,5},{5,6},{6,7},{7,4},{8,9},{9,10},{10,1... | collective-permute-start | bytes 393224 | tf_op jit(solution)/shard_map/ppermute | solution.py:28
